TPU v7x, 32 devices: a whole 2x2x4 slice. The times are simulated.
32 devices in a mesh: dom: 8 (over y, x, core), feat: 4 (over z).
Axes of the slice: x: 2, y: 2, z: 4, core: 2. Of those that a mesh axis runs over, the one named last changes fastest.
Arguments:
- features: bfloat16 [128, 131072], P('feat', 'dom'), may hold values from -6 to 6
- seed_rows: int32 [2048], P('dom'), may hold values from 0 to 16383
- want_rows: int32 [8, 8, 128], P('dom'), may hold values from 0 to 16383
- live_counts: int32 [8, 8], P('dom'), may hold values from 1 to 128, as said below
- hop_one: int32 [15, 2048], P(None, 'dom'), may hold values from 0 to 1023, as said below
- hop_two: int32 [10, 15, 2048], P(None, None, 'dom'), may hold values from 0 to 1023, as said below
- w1_self: bfloat16 [256, 128], replicated, may hold values from -0.5 to 0.5
- w1_neigh: bfloat16 [256, 128], replicated, may hold values from -0.5 to 0.5
- b1: float32 [256], P('feat'), may hold values from -4 to 4
- w2_self: bfloat16 [256, 256], P(None, 'feat'), may hold values from -0.375 to 0.375
- w2_neigh: bfloat16 [256, 256], P(None, 'feat'), may hold values from -0.375 to 0.375
- b2: float32 [256], P('feat'), may hold values from -4 to 4
Outputs:
- embed: float32 [256, 2048], P('feat', 'dom')
Inputs may be any that keep to these rules, and one draw needn't show every extreme that they name: `want_rows`: slots at or beyond live_counts[r, o] are ignored. `live_counts`: in every draw a quarter of the owners, every fourth one from a drawn offset, receive all 128 slots from every requester. `hop_one`: each entry is o * 128 + c, a position in the buffer of the requester that holds seed s, with c < live_counts of that requester and owner o. `hop_two`: each entry is o * 128 + c, a position in the buffer of the requester that holds seed s, with c < live_counts of that requester and owner o.
All inputs are finite; a program needn't handle non-finite values.
Results may differ from a plain program's by a relative error of at most 0.00036.
Values may be sent and summed in bfloat16 or wider, within the bound.
A program may use at most 64 MiB of HBM per device.

v0:
```python
import jax
import jax.numpy as jnp
from jax import lax
from jax.sharding import PartitionSpec as P

OUT = 256
FAN1 = 15
FAN2 = 10
CAP = 128


def aggregate_counts(fetched, hop_one, hop_two):
    feat_dev, slots = fetched.shape
    width = CAP * 4
    first = hop_one.reshape(1, -1)
    second = hop_two.reshape(FAN2, -1)
    columns = first.shape[1]

    def add_block(blocks, carry):
        start = blocks * width
        piece = lax.dynamic_slice_in_dim(fetched, start, width, 1)
        place = start + lax.broadcasted_iota(jnp.int32, (width, 1), 0)
        pick_one = (first == place).astype(jnp.bfloat16)
        pick_two = jnp.zeros((width, columns), jnp.bfloat16)
        for sample in range(FAN2):
            pick_two = pick_two + (second[sample : sample + 1] == place).astype(jnp.bfloat16)
        own_sum = carry[0] + jnp.dot(piece, pick_one, preferred_element_type=jnp.float32)
        mean_sum = carry[1] + jnp.dot(piece, pick_two, preferred_element_type=jnp.float32)
        return (own_sum, mean_sum)

    zeros = jnp.zeros((feat_dev, columns), jnp.float32)
    own_sum, mean_sum = lax.fori_loop(0, slots // width, add_block, (zeros, zeros))
    return (own_sum.astype(jnp.bfloat16), (mean_sum * (1.0 / FAN2)).astype(jnp.bfloat16))


def per_device(
    features,
    seed_rows,
    want_rows,
    live_counts,
    hop_one,
    hop_two,
    w1_self,
    w1_neigh,
    b1,
    w2_self,
    w2_neigh,
    b2,
):
    feat_dev = features.shape[0]
    seed_dev = seed_rows.shape[0]
    hid_dev = b1.shape[0]
    served = jnp.take(
        features,
        lax.all_to_all(want_rows, "dom", split_axis=1, concat_axis=0, tiled=True)[:, 0, :],
        axis=1,
    )
    returned = lax.all_to_all(served, "dom", split_axis=1, concat_axis=1, tiled=True)
    slot_ids = lax.broadcasted_iota(jnp.int32, (1, returned.shape[2]), 1)
    live_slots = slot_ids < live_counts[0][:, None]
    fetched = jnp.where(live_slots[None], returned, jnp.zeros((), jnp.bfloat16)).reshape(
        feat_dev, -1
    )
    x_one, m_two = aggregate_counts(fetched, hop_one, hop_two)
    x_seed = jnp.take(features, seed_rows, axis=1)
    m_one = jnp.sum(x_one.reshape(feat_dev, FAN1, seed_dev), axis=1, dtype=jnp.float32)
    m_one = (m_one * (1.0 / FAN1)).astype(jnp.bfloat16)
    selves = jnp.concatenate([x_one, x_seed], axis=1)
    means = jnp.concatenate([m_two, m_one], axis=1)
    hid_start = lax.axis_index("feat") * hid_dev
    self_rows = lax.dynamic_slice_in_dim(w1_self, hid_start, hid_dev, 0)
    neigh_rows = lax.dynamic_slice_in_dim(w1_neigh, hid_start, hid_dev, 0)
    self_part = self_rows
    neigh_part = neigh_rows
    total = jnp.dot(
        self_part,
        lax.all_gather(selves, "feat", axis=0, tiled=True),
        preferred_element_type=jnp.float32,
    )
    pre = total + jnp.dot(
        neigh_part,
        lax.all_gather(means, "feat", axis=0, tiled=True),
        preferred_element_type=jnp.float32,
    )
    hidden = jnp.maximum(pre + b1[:, None], 0.0)
    hop_cols = FAN1 * seed_dev
    h_one = hidden[:, :hop_cols]
    h_seed = hidden[:, hop_cols:]
    g_mean = jnp.sum(h_one.reshape(hid_dev, FAN1, seed_dev), axis=1) * (1.0 / FAN1)
    second_self = w2_self.astype(jnp.float32)
    second_neigh = w2_neigh.astype(jnp.float32)
    self_part = second_self
    neigh_part = second_neigh
    total = jnp.dot(
        self_part, h_seed, precision=lax.Precision.HIGHEST, preferred_element_type=jnp.float32
    )
    z_out = (
        lax.psum_scatter(
            total
            + jnp.dot(
                neigh_part,
                g_mean,
                precision=lax.Precision.HIGHEST,
                preferred_element_type=jnp.float32,
            ),
            "feat",
            scatter_dimension=0,
            tiled=True,
        )
        + b2[:, None]
    )
    square = lax.psum(jnp.sum(z_out * z_out, axis=0), "feat")
    return z_out * lax.rsqrt(square * (1.0 / OUT) + 1.0)


def solution(mesh):
    return jax.shard_map(
        per_device,
        mesh=mesh,
        in_specs=(
            P("feat", "dom"),
            P("dom"),
            P("dom", None, None),
            P("dom", None),
            P(None, "dom"),
            P(None, None, "dom"),
            P(),
            P(),
            P("feat"),
            P(None, "feat"),
            P(None, "feat"),
            P("feat"),
        ),
        out_specs=P("feat", "dom"),
        check_vma=False,
    )
```

profile of v0, /device:TPU:0, one launch (start us, length us, event | category | flops | bytes accessed | tf_op | source)
XLA Modules:
  0.0 154.3 jit_solution(16646595926999399263)
XLA Ops:
  6.5 5.3 %all-to-all-start = ((s32[1,8,128]{2,0,1:T(1,128)}), s32[1,8,128]{2,0,1:T(1,128)S(1)}, u32[]{:S(2)}, u32[]{:S(2)}) async-start(s32[1,8,128]{2,0,1:T(1,128)} %bitcast.38), calls=%async_computation | async-start | bytes 8192 | tf_op jit(solution)/shard_map/all_to_all | solution.py:55
  11.9 0.7 compare_select_fusion.2
  12.6 0.7 compare_and_fusion.1
  13.2 4.6 %copy.30 = bf16[32,16384]{0,1:T(8,128)(2,1)} copy(bf16[32,16384]{1,0:T(8,128)(2,1)} %param.14) | data formatting | bytes 2097152 | tf_op args[0]
  17.8 3.5 %gather_fusion.1 = bf16[256,32]{1,0:T(8,128)(2,1)S(1)} fusion(bf16[32,16384]{0,1:T(8,128)(2,1)} %copy.30, s32[1024]{0:T(1024)S(1)} %pad_clamp_fusion), kind=kCustom, calls=%fused_computation.1 | custom fusion | bytes 33792 | tf_op jit(solution)/shard_map/jit(_take)/gather | solution.py:65
  21.4 5.6 %gather_fusion = bf16[1024,32]{1,0:T(8,128)(2,1)S(1)} fusion(bf16[32,16384]{0,1:T(8,128)(2,1)} %copy.30, s32[1024]{0:T(1024)S(1)} %fusion.43), kind=kCustom, calls=%fused_computation | custom fusion | bytes 135168 | tf_op jit(solution)/shard_map/jit(_take)/gather | solution.py:53
  27.2 0.6 select_bitcast_fusion.1
  27.8 4.2 %all-to-all-start.1 = ((bf16[32,8,128]{2,0,1:T(8,128)(2,1)}), bf16[32,8,128]{2,0,1:T(8,128)(2,1)S(1)}, u32[]{:S(2)}, u32[]{:S(2)}) async-start(bf16[32,8,128]{2,0,1:T(8,128)(2,1)} %select_bitcast_fusion.1), calls=%async_computation.1 | async-start | bytes 131072 | tf_op jit(solution)/shard_map/all_to_all | solution.py:58
  32.0 0.2 all-gather.3.cloned.1.call-start
  32.6 4.4 %all-to-all-done.1 = bf16[32,8,128]{2,0,1:T(8,128)(2,1)S(1)} async-done(((bf16[32,8,128]{2,0,1:T(8,128)(2,1)}), bf16[32,8,128]{2,0,1:T(8,128)(2,1)S(1)}, u32[]{:S(2)}, u32[]{:S(2)}) %all-to-all-start.1) | async-done | bytes 65568 | tf_op jit(solution)/shard_map/all_to_all | solution.py:58
  37.1 19.3 %while.16 = (s32[]{:T(128)}, f32[32,3840]{1,0:T(8,128)S(1)}, f32[32,3840]{1,0:T(8,128)S(1)}, bf16[32,1024]{1,0:T(8,128)(2,1)S(1)}, s32[1,3840]{1,0:T(1,128)S(1)}...) while((s32[]{:T(128)}, f32[32,3840]{1,0:T(8,128)S(1)}, ...), condition=%wide.region_1.2_spmd.clone, body=%wide.region_0.1_spmd.clone.sunk | while | flops 311132672 | bytes 2556086 | solution.py:32
  37.1 1.5 fusion.60
  38.6 0.4 slice_reduce_fusion.11
  39.0 7.7 %convolution_add_fusion.4 = f32[32,3840]{1,0:T(8,128)S(1)} fusion(s32[3840]{0:T(1024)S(1)} %get-tuple-element.207, s32[3840]{0:T(1024)S(1)} %get-tuple-element.208, s32[3840]{0:T(1024)S(1)} %get-tuple-element.209, s32[3840]{0:T(1024)S(1)} %get-tuple-element.210, s32[3840]{0:T(1024)S(1)} %get-tuple-element.211, s32[3840]{0:T(1024)S(1)} %get-tuple-element.212, ...), kind=kOutput, calls=%fused_computation.14.clone.1 | convolution fusion | flops 183091200 | bytes 1181701 | tf_op jit(solution)/shard_map/while/body/eval_jaxpr/dot_general | solution.py:28
  46.8 1.5 fusion.60
  48.3 0.4 slice_reduce_fusion.11
  48.7 7.7 %convolution_add_fusion.4 = f32[32,3840]{1,0:T(8,128)S(1)} fusion(s32[3840]{0:T(1024)S(1)} %get-tuple-element.207, s32[3840]{0:T(1024)S(1)} %get-tuple-element.208, s32[3840]{0:T(1024)S(1)} %get-tuple-element.209, s32[3840]{0:T(1024)S(1)} %get-tuple-element.210, s32[3840]{0:T(1024)S(1)} %get-tuple-element.211, s32[3840]{0:T(1024)S(1)} %get-tuple-element.212, ...), kind=kOutput, calls=%fused_computation.14.clone.1 | convolution fusion | flops 183091200 | bytes 1181701 | tf_op jit(solution)/shard_map/while/body/eval_jaxpr/dot_general | solution.py:28
  56.5 0.2 reshape.90
  56.7 0.7 pad_maximum_fusion
  57.7 0.7 pad_maximum_fusion.1
  58.5 26.5 %all-gather.3.cloned.1.call-done = bf16[128,4096]{1,0:T(8,128)(2,1)} async-done(((bf16[32,4096]{1,0:T(8,128)(2,1)}), bf16[128,4096]{1,0:T(8,128)(2,1)}) %all-gather.3.cloned.1.call-update) | async-done | bytes 1048592 | tf_op jit(solution)/shard_map/all_gather | solution.py:77
  84.9 1.5 fusion.40
  86.5 27.4 %all-gather.5.cloned.1.call-done = bf16[128,4096]{1,0:T(8,128)(2,1)} async-done(((bf16[32,4096]{1,0:T(8,128)(2,1)}), bf16[128,4096]{1,0:T(8,128)(2,1)}) %all-gather.5.cloned.1.call-update) | async-done | bytes 1048592 | tf_op jit(solution)/shard_map/all_gather | solution.py:82
  113.9 1.5 fusion.33
  115.5 0.3 fusion.35
  115.9 0.3 reshape.89
  116.4 0.3 fusion.34
  116.7 0.8 copy.36
  117.5 19.5 %reduce-scatter.4.cloned.1.call-done = f32[64,256]{1,0:T(8,128)} async-done(((f32[256,256]{1,0:T(8,128)}), f32[64,256]{1,0:T(8,128)}) %reduce-scatter.4.cloned.1.call-update) | async-done | bytes 65552
  137.1 0.9 copy.37
  138.1 8.8 %psum.7 = f32[256]{0:T(256)S(1)} all-reduce(f32[256]{0:T(256)S(1)} %multiply_reduce_fusion), channel_id=1, replica_groups=mesh['dom'=8,'feat'=4] {'feat'}, use_global_device_ids=true, to_apply=%region_6.7 | all-reduce | flops 256 | bytes 2048 | tf_op jit(solution)/shard_map/psum | solution.py:112
  147.1 0.7 copy.35
  (48 shorter events, 1.5 us)
Async XLA Ops:
  6.5 78.4 %copy-start = (bf16[256,128]{1,0:T(8,128)(2,1)S(1)}, bf16[256,128]{1,0:T(8,128)(2,1)}, u32[]{:S(2)}) copy-start(bf16[256,128]{1,0:T(8,128)(2,1)} %param.20) | copy-start | bytes 196612
  6.5 25.7 %copy-start.7 = (s32[1,8]{1,0:T(1,128)S(1)}, s32[1,8]{1,0:T(1,128)}, u32[]{:S(2)}) copy-start(s32[1,8]{1,0:T(1,128)} %param.17) | copy-start | bytes 100
  6.5 25.9 %copy-start.4 = (s32[15,256]{1,0:T(8,128)S(1)}, s32[15,256]{1,0:T(8,128)}, u32[]{:S(2)}) copy-start(s32[15,256]{1,0:T(8,128)} %param.18) | copy-start | bytes 46084
  6.5 25.9 %copy-start.1 = (s32[10,15,256]{2,1,0:T(8,128)S(1)}, s32[10,15,256]{2,1,0:T(8,128)}, u32[]{:S(2)}) copy-start(s32[10,15,256]{2,1,0:T(8,128)} %param.19) | copy-start | bytes 460804
  6.5 14.9 %all-to-all-start = ((s32[1,8,128]{2,0,1:T(1,128)}), s32[1,8,128]{2,0,1:T(1,128)S(1)}, u32[]{:S(2)}, u32[]{:S(2)}) async-start(s32[1,8,128]{2,0,1:T(1,128)} %bitcast.38), calls=%async_computation | async-start | bytes 8192 | tf_op jit(solution)/shard_map/all_to_all | solution.py:55
  27.8 9.2 %all-to-all-start.1 = ((bf16[32,8,128]{2,0,1:T(8,128)(2,1)}), bf16[32,8,128]{2,0,1:T(8,128)(2,1)S(1)}, u32[]{:S(2)}, u32[]{:S(2)}) async-start(bf16[32,8,128]{2,0,1:T(8,128)(2,1)} %select_bitcast_fusion.1), calls=%async_computation.1 | async-start | bytes 131072 | tf_op jit(solution)/shard_map/all_to_all | solution.py:58
  32.0 52.9 %all-gather.3.cloned.1.call-start = ((), (), s32[]{:S(2)}) async-start(), calls=%async_computation.3 | async-start | bytes 1310720 | tf_op jit(solution)/shard_map/all_gather | solution.py:77
  56.4 57.5 %copy-start.6 = (f32[64]{0:T(128)S(1)}, f32[64]{0:T(128)}, u32[]{:S(2)}) copy-start(f32[64]{0:T(128)} %param.22) | copy-start | bytes 772
  57.4 56.5 %all-gather.5.cloned.1.call-start = ((), (), s32[]{:S(2)}) async-start(), calls=%async_computation.4 | async-start | bytes 1310720 | tf_op jit(solution)/shard_map/all_gather | solution.py:82
  57.6 57.9 %copy-start.3 = (bf16[256,64]{0,1:T(8,128)(2,1)S(1)}, bf16[256,64]{0,1:T(8,128)(2,1)}, u32[]{:S(2)}) copy-start(bf16[256,64]{0,1:T(8,128)(2,1)} %param.23) | copy-start | bytes 98308
  58.4 78.7 %reduce-scatter.4.cloned.1.call-start = ((), (), s32[]{:S(2)}) async-start(), calls=%async_computation.5 | async-start | bytes 327680
  86.4 29.9 %copy-start.2 = (bf16[256,64]{0,1:T(8,128)(2,1)S(1)}, bf16[256,64]{0,1:T(8,128)(2,1)}, u32[]{:S(2)}) copy-start(bf16[256,64]{0,1:T(8,128)(2,1)} %param.24) | copy-start | bytes 98308
  115.4 22.6 %copy-start.5 = (f32[64]{0:T(128)S(1)}, f32[64]{0:T(128)}, u32[]{:S(2)}) copy-start(f32[64]{0:T(128)} %param.25) | copy-start | bytes 772
Sparse Core Ops, SparseCore 0:
  57.5 27.3 all-gather.2
  86.5 27.3 all-gather.4
  117.7 19.3 reduce-scatter.3
where the time goes:
time: 155 us; the launch traced here: 154 us
  waiting for transfers between devices  77.9 us (50%)
  matrix products  22 us (14%)
  local copies, waits for them, and re-layouts  17.9 us (12%)
  between operations  13.4 us (9%)
  starting transfers between devices  9.84 us (6%)
  blocking collectives  8.85 us (6%)
  other arithmetic  4.35 us (3%)
    all_gather x1, waiting for transfers between devices, per_device(): lax.all_gather(means, 'feat', axis=0, tiled=True)  27.4 us
    all_gather x1, waiting for transfers between devices, per_device(): lax.all_gather(selves, 'feat', axis=0, tiled=True)  26.5 us
    unnamed x4, waiting for transfers between devices  19.6 us
    dot_general x2, matrix products, add_block(): jnp.dot(piece, pick_two, preferred_element_type=jnp.float32)  15.4 us
    psum x1, blocking collectives, per_device(): square = lax.psum(jnp.sum(z_out * z_out, axis=0), 'feat')  8.85 us
    unnamed x22, local copies, waits for them, and re-layouts  6.56 us
    gather x2, local copies, waits for them, and re-layouts, per_device(): jnp.take(features, lax.all_to_all(want_rows, 'dom', split_axis=1, concat_...  5.73 us
    all_to_all x1, starting transfers between devices, per_device(): lax.all_to_all(want_rows, 'dom', split_axis=1, concat_axis=0, tiled=True)  5.34 us
  transfers between devices with their start and end apart: 5, of which 4 were waited for; matrix products, arithmetic and copies ran while one was open for 8% of the time, Pallas kernels for 0%

commit v1 on v0

--- a/solution.py
+++ b/solution.py
@@ -7,6 +7,13 @@
 FAN1 = 15
 FAN2 = 10
 CAP = 128
+
+
+def trade_parts(x, axis, split, join):
+    size = lax.axis_size(axis)
+    shards = jnp.stack(jnp.split(x, size, axis=split), axis=0)
+    shards = lax.all_to_all(shards, axis, split_axis=0, concat_axis=0)
+    return jnp.concatenate(shards, axis=join)
 
 
 def aggregate_counts(fetched, hop_one, hop_two):
@@ -55,7 +62,7 @@
         lax.all_to_all(want_rows, "dom", split_axis=1, concat_axis=0, tiled=True)[:, 0, :],
         axis=1,
     )
-    returned = lax.all_to_all(served, "dom", split_axis=1, concat_axis=1, tiled=True)
+    returned = trade_parts(served, "dom", 1, 1)
     slot_ids = lax.broadcasted_iota(jnp.int32, (1, returned.shape[2]), 1)
     live_slots = slot_ids < live_counts[0][:, None]
     fetched = jnp.where(live_slots[None], returned, jnp.zeros((), jnp.bfloat16)).reshape(

time: 155 us -> 160 us (1.032)
  local copies, waits for them, and re-layouts: 17.9 us -> 23.4 us
    unnamed x22 -> x27, local copies, waits for them, and re-layouts: 6.56 us -> 10.7 us
  transfers between devices with their start and end apart: 5 -> 5, of which waited for: 4 -> 4; matrix products, arithmetic and copies ran while one was open for 8% -> 6% of each run, Pallas kernels for 0% -> 0%
where the time goes in v1:
time: 160 us; the launch traced here: 159 us
  waiting for transfers between devices  78.1 us (49%)
  local copies, waits for them, and re-layouts  23.4 us (15%)
  matrix products  22 us (14%)
  between operations  13.4 us (8%)
  starting transfers between devices  9.83 us (6%)
  blocking collectives  8.75 us (5%)
  other arithmetic  3.66 us (2%)
    all_gather x1, waiting for transfers between devices, per_device(): lax.all_gather(means, 'feat', axis=0, tiled=True)  27.4 us
    all_gather x1, waiting for transfers between devices, per_device(): lax.all_gather(selves, 'feat', axis=0, tiled=True)  26.5 us
    unnamed x4, waiting for transfers between devices  19.6 us
    dot_general x2, matrix products, add_block(): jnp.dot(piece, pick_two, preferred_element_type=jnp.float32)  15.4 us
    unnamed x27, local copies, waits for them, and re-layouts  10.7 us
    psum x1, blocking collectives, per_device(): square = lax.psum(jnp.sum(z_out * z_out, axis=0), 'feat')  8.75 us
    gather x2, local copies, waits for them, and re-layouts, per_device(): jnp.take(features, lax.all_to_all(want_rows, 'dom', split_axis=1, concat_...  5.73 us
    all_to_all x1, starting transfers between devices, per_device(): lax.all_to_all(want_rows, 'dom', split_axis=1, concat_axis=0, tiled=True)  5.33 us
  transfers between devices with their start and end apart: 5, of which 4 were waited for; matrix products, arithmetic and copies ran while one was open for 6% of the time, Pallas kernels for 0%

profile of v1, /device:TPU:0, one launch (start us, length us, event | category | flops | bytes accessed | tf_op | source)
XLA Modules:
  0.0 159.3 jit_solution(15556391468556259631)
XLA Ops:
  6.5 5.3 %all-to-all-start = ((s32[1,8,128]{2,0,1:T(1,128)}), s32[1,8,128]{2,0,1:T(1,128)S(1)}, u32[]{:S(2)}, u32[]{:S(2)}) async-start(s32[1,8,128]{2,0,1:T(1,128)} %bitcast.77), calls=%async_computation | async-start | bytes 8192 | tf_op jit(solution)/shard_map/all_to_all | solution.py:62
  11.9 0.7 compare_select_fusion.2
  12.6 0.7 lt.69
  13.3 0.7 compare_and_fusion.1
  14.0 4.6 %copy.30 = bf16[32,16384]{0,1:T(8,128)(2,1)} copy(bf16[32,16384]{1,0:T(8,128)(2,1)} %param.14) | data formatting | bytes 2097152 | tf_op args[0]
  18.8 3.5 %gather_fusion.1 = bf16[256,32]{1,0:T(8,128)(2,1)S(1)} fusion(bf16[32,16384]{0,1:T(8,128)(2,1)} %copy.30, s32[1024]{0:T(1024)S(1)} %get-tuple-element.161), kind=kCustom, calls=%fused_computation.1 | custom fusion | bytes 33792 | tf_op jit(solution)/shard_map/jit(_take)/gather | solution.py:72
  22.3 5.6 %gather_fusion = bf16[1024,32]{1,0:T(8,128)(2,1)S(1)} fusion(bf16[32,16384]{0,1:T(8,128)(2,1)} %copy.30, s32[1024]{0:T(1024)S(1)} %get-tuple-element.160), kind=kCustom, calls=%fused_computation | custom fusion | bytes 135168 | tf_op jit(solution)/shard_map/jit(_take)/gather | solution.py:60
  28.0 0.6 constant_dynamic-update-slice_fusion.7
  28.6 0.6 constant_dynamic-update-slice_fusion.6
  29.2 0.6 constant_dynamic-update-slice_fusion.5
  29.8 0.6 constant_dynamic-update-slice_fusion.4
  30.4 0.6 constant_dynamic-update-slice_fusion.3
  31.0 0.6 constant_dynamic-update-slice_fusion.2
  32.2 0.6 constant_dynamic-update-slice_fusion
  32.8 4.2 %all-to-all-start.1 = ((bf16[8,32,1,128]{3,1,2,0:T(8,128)(2,1)}), bf16[8,32,1,128]{3,1,2,0:T(8,128)(2,1)S(1)}, u32[]{:S(2)}, u32[]{:S(2)}) async-start(bf16[8,32,1,128]{3,1,2,0:T(8,128)(2,1)} %constant_dynamic-update-slice_fusion), calls=%async_computation.1 | async-start | bytes 131072 | tf_op jit(solution)/shard_map/all_to_all | solution.py:15
  37.4 4.6 %all-to-all-done.1 = bf16[8,32,1,128]{3,1,2,0:T(8,128)(2,1)S(1)} async-done(((bf16[8,32,1,128]{3,1,2,0:T(8,128)(2,1)}), bf16[8,32,1,128]{3,1,2,0:T(8,128)(2,1)S(1)}, u32[]{:S(2)}, u32[]{:S(2)}) %all-to-all-start.1) | async-done | bytes 65568 | tf_op jit(solution)/shard_map/all_to_all | solution.py:15
  42.1 19.3 %while.16 = (s32[]{:T(128)}, f32[32,3840]{1,0:T(8,128)S(1)}, f32[32,3840]{1,0:T(8,128)S(1)}, bf16[32,1024]{1,0:T(8,128)(2,1)S(1)}, s32[1,3840]{1,0:T(1,128)S(1)}...) while((s32[]{:T(128)}, f32[32,3840]{1,0:T(8,128)S(1)}, ...), condition=%wide.region_1.2_spmd.clone, body=%wide.region_0.1_spmd.clone.sunk | while | flops 311132672 | bytes 2556086 | solution.py:39
  42.2 1.5 fusion.60
  44.1 7.7 %convolution_add_fusion.4 = f32[32,3840]{1,0:T(8,128)S(1)} fusion(s32[3840]{0:T(1024)S(1)} %get-tuple-element.209, s32[3840]{0:T(1024)S(1)} %get-tuple-element.210, s32[3840]{0:T(1024)S(1)} %get-tuple-element.211, s32[3840]{0:T(1024)S(1)} %get-tuple-element.212, s32[3840]{0:T(1024)S(1)} %get-tuple-element.213, s32[3840]{0:T(1024)S(1)} %get-tuple-element.214, ...), kind=kOutput, calls=%fused_computation.14.clone.1 | convolution fusion | flops 183091200 | bytes 1181701 | tf_op jit(solution)/shard_map/while/body/eval_jaxpr/dot_general | solution.py:35
  51.9 1.5 fusion.60
  53.7 7.7 %convolution_add_fusion.4 = f32[32,3840]{1,0:T(8,128)S(1)} fusion(s32[3840]{0:T(1024)S(1)} %get-tuple-element.209, s32[3840]{0:T(1024)S(1)} %get-tuple-element.210, s32[3840]{0:T(1024)S(1)} %get-tuple-element.211, s32[3840]{0:T(1024)S(1)} %get-tuple-element.212, s32[3840]{0:T(1024)S(1)} %get-tuple-element.213, s32[3840]{0:T(1024)S(1)} %get-tuple-element.214, ...), kind=kOutput, calls=%fused_computation.14.clone.1 | convolution fusion | flops 183091200 | bytes 1181701 | tf_op jit(solution)/shard_map/while/body/eval_jaxpr/dot_general | solution.py:35
  61.7 0.7 pad_maximum_fusion
  62.7 0.7 pad_maximum_fusion.1
  63.5 26.5 %all-gather.3.cloned.1.call-done = bf16[128,4096]{1,0:T(8,128)(2,1)} async-done(((bf16[32,4096]{1,0:T(8,128)(2,1)}), bf16[128,4096]{1,0:T(8,128)(2,1)}) %all-gather.3.cloned.1.call-update) | async-done | bytes 1048592 | tf_op jit(solution)/shard_map/all_gather | solution.py:84
  90.0 1.5 fusion.40
  91.5 27.4 %all-gather.5.cloned.1.call-done = bf16[128,4096]{1,0:T(8,128)(2,1)} async-done(((bf16[32,4096]{1,0:T(8,128)(2,1)}), bf16[128,4096]{1,0:T(8,128)(2,1)}) %all-gather.5.cloned.1.call-update) | async-done | bytes 1048592 | tf_op jit(solution)/shard_map/all_gather | solution.py:89
  118.9 1.5 fusion.33
  121.7 0.8 copy.36
  122.6 19.5 %reduce-scatter.4.cloned.1.call-done = f32[64,256]{1,0:T(8,128)} async-done(((f32[256,256]{1,0:T(8,128)}), f32[64,256]{1,0:T(8,128)}) %reduce-scatter.4.cloned.1.call-update) | async-done | bytes 65552
  142.1 0.9 copy.37
  143.2 8.8 %psum.7 = f32[256]{0:T(256)S(1)} all-reduce(f32[256]{0:T(256)S(1)} %multiply_reduce_fusion), channel_id=1, replica_groups=mesh['dom'=8,'feat'=4] {'feat'}, use_global_device_ids=true, to_apply=%region_6.7 | all-reduce | flops 256 | bytes 2048 | tf_op jit(solution)/shard_map/psum | solution.py:119
  152.0 0.7 copy.35
  (55 shorter events, 4.2 us)
Async XLA Ops:
  6.5 83.4 %copy-start = (bf16[256,128]{1,0:T(8,128)(2,1)S(1)}, bf16[256,128]{1,0:T(8,128)(2,1)}, u32[]{:S(2)}) copy-start(bf16[256,128]{1,0:T(8,128)(2,1)} %param.20) | copy-start | bytes 196612
  6.5 12.0 %copy-start.4 = (s32[15,256]{1,0:T(8,128)S(1)}, s32[15,256]{1,0:T(8,128)}, u32[]{:S(2)}) copy-start(s32[15,256]{1,0:T(8,128)} %param.18) | copy-start | bytes 46084
  6.5 12.0 %copy-start.1 = (s32[10,15,256]{2,1,0:T(8,128)S(1)}, s32[10,15,256]{2,1,0:T(8,128)}, u32[]{:S(2)}) copy-start(s32[10,15,256]{2,1,0:T(8,128)} %param.19) | copy-start | bytes 460804
  6.5 12.2 %all-to-all-start = ((s32[1,8,128]{2,0,1:T(1,128)}), s32[1,8,128]{2,0,1:T(1,128)S(1)}, u32[]{:S(2)}, u32[]{:S(2)}) async-start(s32[1,8,128]{2,0,1:T(1,128)} %bitcast.77), calls=%async_computation | async-start | bytes 8192 | tf_op jit(solution)/shard_map/all_to_all | solution.py:62
  32.8 9.2 %all-to-all-start.1 = ((bf16[8,32,1,128]{3,1,2,0:T(8,128)(2,1)}), bf16[8,32,1,128]{3,1,2,0:T(8,128)(2,1)S(1)}, u32[]{:S(2)}, u32[]{:S(2)}) async-start(bf16[8,32,1,128]{3,1,2,0:T(8,128)(2,1)} %constant_dynamic-update-slice_fusion), calls=%async_computation.1 | async-start | bytes 131072 | tf_op jit(solution)/shard_map/all_to_all | solution.py:15
  37.0 52.9 %all-gather.3.cloned.1.call-start = ((), (), s32[]{:S(2)}) async-start(), calls=%async_computation.3 | async-start | bytes 1310720 | tf_op jit(solution)/shard_map/all_gather | solution.py:84
  61.5 57.5 %copy-start.6 = (f32[64]{0:T(128)S(1)}, f32[64]{0:T(128)}, u32[]{:S(2)}) copy-start(f32[64]{0:T(128)} %param.22) | copy-start | bytes 772
  62.5 56.5 %all-gather.5.cloned.1.call-start = ((), (), s32[]{:S(2)}) async-start(), calls=%async_computation.4 | async-start | bytes 1310720 | tf_op jit(solution)/shard_map/all_gather | solution.py:89
  62.7 57.9 %copy-start.3 = (bf16[256,64]{0,1:T(8,128)(2,1)S(1)}, bf16[256,64]{0,1:T(8,128)(2,1)}, u32[]{:S(2)}) copy-start(bf16[256,64]{0,1:T(8,128)(2,1)} %param.23) | copy-start | bytes 98308
  63.4 78.7 %reduce-scatter.4.cloned.1.call-start = ((), (), s32[]{:S(2)}) async-start(), calls=%async_computation.5 | async-start | bytes 327680
  91.5 29.9 %copy-start.2 = (bf16[256,64]{0,1:T(8,128)(2,1)S(1)}, bf16[256,64]{0,1:T(8,128)(2,1)}, u32[]{:S(2)}) copy-start(bf16[256,64]{0,1:T(8,128)(2,1)} %param.24) | copy-start | bytes 98308
  120.5 22.6 %copy-start.5 = (f32[64]{0:T(128)S(1)}, f32[64]{0:T(128)}, u32[]{:S(2)}) copy-start(f32[64]{0:T(128)} %param.25) | copy-start | bytes 772
Sparse Core Ops, SparseCore 0:
  62.6 27.3 all-gather.2
  91.5 27.3 all-gather.4
  122.7 19.3 reduce-scatter.3
